TPU v7x, 32 devices: a whole 2x2x4 slice. The times are simulated.
32 devices in a mesh: row: 4 (over z), col: 8 (over y, x, core).
Axes of the slice: x: 2, y: 2, z: 4, core: 2. Of those that a mesh axis runs over, the one named last changes fastest.
Arguments:
- factor_wide: float32 [4, 4, 2, 8, 512, 512], P(None, 'row', None, 'col'), may hold values from -1 to 2, as said below
- factor_narrow: bfloat16 [4, 4, 2, 8, 512, 512], P(None, 'row', None, 'col'), may hold values from -1 to 2, as said below
- flags: int32 [4, 4, 2, 8], P(None, 'row', None, 'col'), may hold values from 0 to 1
- forward_solution: float32 [2, 8, 512, 128], P(None, 'col'), may hold values from -0.5 to 0.5
- solution_grad: float32 [2, 8, 512, 128], P(None, 'col'), may hold values from -1.8 to 1.8
Outputs:
- rhs_grad: float32 [4, 4, 512, 128], P(None, 'row')
- factor_grad: float32 [4, 4, 2, 8, 512, 512], P(None, 'row', None, 'col')
Inputs may be any that keep to these rules, and one draw needn't show every extreme that they name: `factor_wide`: the diagonal entries of every diagonal tile lie between 1 and 2. `factor_narrow`: the diagonal entries of every diagonal tile lie between 1 and 2.
All inputs are finite; a program needn't handle non-finite values.
Results may differ from a plain program's by a relative error of at most 0.0003.
Values sent between devices are 32-bit elements; how exact they have to be, the bound alone decides.
A program may use at most 64 MiB of HBM per device.

v0:
```python
import jax
import jax.numpy as jnp
from jax import lax
from jax.sharding import PartitionSpec as P

HIGHEST_PRECISION = lax.Precision.HIGHEST


def broadcast(value, axis, root):
    mine = lax.axis_index(axis) == root
    return lax.psum(jnp.where(mine, value, jnp.zeros_like(value)), axis)


def from_behind(value, axis, by):
    size = lax.axis_size(axis)
    return lax.ppermute(value, axis, [(i, (i + by) % size) for i in range(size)])


def lower_mask(row_index, col_index, tile_width):
    inner_mask = lax.broadcasted_iota(
        jnp.int32, (tile_width, tile_width), 0
    ) >= lax.broadcasted_iota(jnp.int32, (tile_width, tile_width), 1)
    return (row_index > col_index) | (row_index == col_index) & inner_mask


def body(factor_wide, factor_narrow, flags, forward_solution, solution_grad):
    row_count = lax.axis_size("row")
    col_count = lax.axis_size("col")
    my_row = lax.axis_index("row")
    my_col = lax.axis_index("col")
    local_rows = factor_wide.shape[0]
    local_cols = factor_wide.shape[2]
    tile_width = factor_wide.shape[4]
    rhs_width = forward_solution.shape[3]
    tile_count = local_rows * row_count
    factor_tiles = jnp.where(
        flags[:, 0, :, 0, None, None] == 1,
        factor_narrow[:, 0, :, 0].astype(jnp.float32),
        factor_wide[:, 0, :, 0],
    )
    solution_local = forward_solution[:, 0]
    target_local = solution_grad[:, 0]
    row_index = jnp.arange(local_rows, dtype=jnp.int32) * row_count + my_row
    col_index = jnp.arange(local_cols, dtype=jnp.int32) * col_count + my_col
    empty_block = jnp.zeros((tile_width, rhs_width), jnp.float32)

    def nothing_block():
        return empty_block

    def column_partial(rhs_local, target, lowest):

        def on_owner():
            column = lax.dynamic_index_in_dim(factor_tiles, target // col_count, 1, keepdims=False)
            weight = (row_index >= lowest).astype(jnp.float32)
            masked = rhs_local * weight[:, None, None]
            return jnp.einsum("aki,akr->ir", column, masked, precision=HIGHEST_PRECISION)

        return lax.cond(my_col == target % col_count, on_owner, nothing_block)

    def target_block(target):
        return lax.dynamic_index_in_dim(target_local, target // col_count, 0, keepdims=False)

    def advance(right_side, target, carried):
        rhs_local, factor_grad = carried
        local_slot = target // row_count
        holds_row = my_row == target % row_count
        is_owner = holds_row & (my_col == target % col_count)

        def solve_here():
            tile_row = lax.dynamic_index_in_dim(factor_tiles, local_slot, 0, keepdims=False)
            diagonal = lax.dynamic_index_in_dim(tile_row, target // col_count, 0, keepdims=False)
            return lax.linalg.triangular_solve(
                diagonal, right_side, left_side=True, lower=True, transpose_a=True
            )

        solved = lax.cond(is_owner, solve_here, nothing_block)
        arrived = broadcast(solved, "col", target % col_count)
        current = lax.dynamic_index_in_dim(rhs_local, local_slot, 0, keepdims=False)
        rhs_local = lax.dynamic_update_index_in_dim(
            rhs_local, jnp.where(holds_row, arrived, current), local_slot, 0
        )
        return (rhs_local, factor_grad)

    final_index = tile_count - 1
    carried = (
        jnp.zeros((local_rows, tile_width, rhs_width), jnp.float32),
        jnp.zeros((local_rows, local_cols, tile_width, tile_width), jnp.float32),
    )
    carried = advance(target_block(jnp.int32(final_index)), jnp.int32(final_index), carried)

    def sweep_step(offset, loop_state):
        carried, early_sum = loop_state
        target = final_index - 1 - offset
        rhs_local = carried[0]
        source = target + 1

        def compute_fresh():
            tile_row = lax.dynamic_index_in_dim(
                factor_tiles, source // row_count, 0, keepdims=False
            )
            tile_now = lax.dynamic_index_in_dim(tile_row, target // col_count, 0, keepdims=False)
            newest = lax.dynamic_index_in_dim(rhs_local, source // row_count, 0, keepdims=False)
            return jnp.dot(
                tile_now.T, newest, precision=HIGHEST_PRECISION, preferred_element_type=jnp.float32
            )

        fresh_owner = (my_row == source % row_count) & (my_col == target % col_count)
        fresh_term = lax.cond(fresh_owner, compute_fresh, nothing_block)
        moved_term = from_behind(fresh_term, "row", -1)
        following = jnp.maximum(target - 1, 0)
        next_partial = column_partial(rhs_local, following, source)
        next_sum = lax.psum(next_partial, "row")
        carried = advance(target_block(target) - early_sum - moved_term, target, carried)
        return (carried, next_sum)

    carried, unused_sum = lax.fori_loop(0, final_index, sweep_step, (carried, empty_block))
    rhs_local, factor_grad = carried
    products = -jnp.einsum("akr,blr->abkl", rhs_local, solution_local, precision=HIGHEST_PRECISION)
    masks = lower_mask(row_index[:, None, None, None], col_index[None, :, None, None], tile_width)
    factor_grad = jnp.where(masks, products, jnp.zeros_like(products))
    return (rhs_local[:, None], factor_grad[:, None, :, None])


def solution(mesh):
    placed = (
        P(None, "row", None, "col", None, None),
        P(None, "row", None, "col", None, None),
        P(None, "row", None, "col"),
        P(None, "col", None, None),
        P(None, "col", None, None),
    )
    return jax.shard_map(
        body,
        mesh=mesh,
        in_specs=placed,
        out_specs=(P(None, "row", None, None), P(None, "row", None, "col", None, None)),
        check_vma=False,
    )
```

profile of v0, /device:TPU:0, one launch (start us, length us, event | category | flops | bytes accessed | tf_op | source)
XLA Modules:
  0.0 2219.2 jit_solution(8826648313586827079)
XLA Ops:
  7.3 9.9 copy.12
  17.2 7.3 copy.11
  24.5 9.6 convert_select_fusion
  35.9 117.2 %all-reduce.5.cloned.1.call-done = f32[512,128]{1,0:T(8,128)} async-done(((f32[512,128]{1,0:T(8,128)}), f32[512,128]{1,0:T(8,128)}) %all-reduce.5.cloned.1.call-update) | async-done | bytes 262160 | tf_op jit(solution)/shard_map/psum | solution.py:11
  153.2 2048.1 %while.28 = (s32[]{:T(128)}, f32[4,512,128]{2,1,0:T(8,128)S(1)}, f32[512,128]{1,0:T(8,128)S(1)}, s32[]{:T(128)}, s32[]{:T(128)}, /*index=5*/f32[4,2,512,512]{2,3...) while((s32[]{:T(128)}, f32[4,512,128]{2,1,0:T(8,128)S(1)}, ...), condition=%wide.region_12.14_spmd.clone.clone, body=%wide.region_3.13_spmd.clone.clone.sunk | while | flops 2266480640 | bytes 54005560 | solution.py:116
  163.3 40.6 %all-reduce.9.cloned.1.call-done = f32[512,128]{1,0:T(8,128)} async-done(((f32[512,128]{1,0:T(8,128)}), f32[512,128]{1,0:T(8,128)}) %all-reduce.9.cloned.1.call-update) | async-done | bytes 262160 | tf_op jit(solution)/shard_map/while/body/eval_jaxpr/psum | solution.py:112
  204.9 86.8 %all-reduce.7.cloned.1.call-done = f32[512,128]{1,0:T(8,128)} async-done(((f32[512,128]{1,0:T(8,128)}), f32[512,128]{1,0:T(8,128)}) %all-reduce.7.cloned.1.call-update) | async-done | bytes 262160 | tf_op jit(solution)/shard_map/while/body/eval_jaxpr/psum | solution.py:11
  300.8 39.6 %all-reduce.9.cloned.1.call-done = f32[512,128]{1,0:T(8,128)} async-done(((f32[512,128]{1,0:T(8,128)}), f32[512,128]{1,0:T(8,128)}) %all-reduce.9.cloned.1.call-update) | async-done | bytes 262160 | tf_op jit(solution)/shard_map/while/body/eval_jaxpr/psum | solution.py:112
  341.4 85.4 %all-reduce.7.cloned.1.call-done = f32[512,128]{1,0:T(8,128)} async-done(((f32[512,128]{1,0:T(8,128)}), f32[512,128]{1,0:T(8,128)}) %all-reduce.7.cloned.1.call-update) | async-done | bytes 262160 | tf_op jit(solution)/shard_map/while/body/eval_jaxpr/psum | solution.py:11
  435.9 40.6 %all-reduce.9.cloned.1.call-done = f32[512,128]{1,0:T(8,128)} async-done(((f32[512,128]{1,0:T(8,128)}), f32[512,128]{1,0:T(8,128)}) %all-reduce.9.cloned.1.call-update) | async-done | bytes 262160 | tf_op jit(solution)/shard_map/while/body/eval_jaxpr/psum | solution.py:112
  477.4 85.9 %all-reduce.7.cloned.1.call-done = f32[512,128]{1,0:T(8,128)} async-done(((f32[512,128]{1,0:T(8,128)}), f32[512,128]{1,0:T(8,128)}) %all-reduce.7.cloned.1.call-update) | async-done | bytes 262160 | tf_op jit(solution)/shard_map/while/body/eval_jaxpr/psum | solution.py:11
  572.6 37.7 %all-reduce.9.cloned.1.call-done = f32[512,128]{1,0:T(8,128)} async-done(((f32[512,128]{1,0:T(8,128)}), f32[512,128]{1,0:T(8,128)}) %all-reduce.9.cloned.1.call-update) | async-done | bytes 262160 | tf_op jit(solution)/shard_map/while/body/eval_jaxpr/psum | solution.py:112
  611.3 88.0 %all-reduce.7.cloned.1.call-done = f32[512,128]{1,0:T(8,128)} async-done(((f32[512,128]{1,0:T(8,128)}), f32[512,128]{1,0:T(8,128)}) %all-reduce.7.cloned.1.call-update) | async-done | bytes 262160 | tf_op jit(solution)/shard_map/while/body/eval_jaxpr/psum | solution.py:11
  709.4 40.6 %all-reduce.9.cloned.1.call-done = f32[512,128]{1,0:T(8,128)} async-done(((f32[512,128]{1,0:T(8,128)}), f32[512,128]{1,0:T(8,128)}) %all-reduce.9.cloned.1.call-update) | async-done | bytes 262160 | tf_op jit(solution)/shard_map/while/body/eval_jaxpr/psum | solution.py:112
  751.0 86.8 %all-reduce.7.cloned.1.call-done = f32[512,128]{1,0:T(8,128)} async-done(((f32[512,128]{1,0:T(8,128)}), f32[512,128]{1,0:T(8,128)}) %all-reduce.7.cloned.1.call-update) | async-done | bytes 262160 | tf_op jit(solution)/shard_map/while/body/eval_jaxpr/psum | solution.py:11
  841.4 5.7 conditional.16
  841.4 5.7 fusion.11
  848.8 37.8 %all-reduce.9.cloned.1.call-done = f32[512,128]{1,0:T(8,128)} async-done(((f32[512,128]{1,0:T(8,128)}), f32[512,128]{1,0:T(8,128)}) %all-reduce.9.cloned.1.call-update) | async-done | bytes 262160 | tf_op jit(solution)/shard_map/while/body/eval_jaxpr/psum | solution.py:112
  887.5 85.3 %all-reduce.7.cloned.1.call-done = f32[512,128]{1,0:T(8,128)} async-done(((f32[512,128]{1,0:T(8,128)}), f32[512,128]{1,0:T(8,128)}) %all-reduce.7.cloned.1.call-update) | async-done | bytes 262160 | tf_op jit(solution)/shard_map/while/body/eval_jaxpr/psum | solution.py:11
  977.3 15.6 collective-permute-done
  992.9 65.2 %conditional.15 = (f32[512,128]{1,0:T(8,128)S(1)}) conditional(s32[]{:T(128)} %convert_element_type.68, () %tuple.144, (s32[]{:T(128)}, s32[]{:T(128)}, f32[4,2,512,512]{2,3,0,1:T(8,128)}, s32[]{:T(128)}, pred[]{:T(512)}, /*index=5*/pred[]{:T(512)}, s32[]{:T(128)}, f32[2,512,128]{2,1,0:T(8,128)}, f32[512,128]{1,0:T(8,128)S(1)}, ...), branch_computations={%region_6.7_spmd, %region_7.8_spmd} | conditional | flops 252690464 | bytes 22546512 | solution.py:76
  992.9 10.0 copy.8
  1004.2 10.6 while.27
  1014.8 40.1 %custom-call.5 = f32[4,128,128]{1,2,0:T(8,128)S(1)} custom-call(f32[4,128,128]{2,1,0:T(8,128)} %get-tuple-element.560), custom_call_target="InvertDiagBlocksLowerTriangular" | custom-call | tf_op jit(solution)/shard_map/while/body/eval_jaxpr/cond/branch_1_fun/triangular_solve/custom-call.1 | solution.py:72
  1059.8 48.9 %all-reduce.7.cloned.1.call-done = f32[512,128]{1,0:T(8,128)} async-done(((f32[512,128]{1,0:T(8,128)}), f32[512,128]{1,0:T(8,128)}) %all-reduce.7.cloned.1.call-update) | async-done | bytes 262160 | tf_op jit(solution)/shard_map/while/body/eval_jaxpr/psum | solution.py:11
  1118.0 37.9 %all-reduce.9.cloned.1.call-done = f32[512,128]{1,0:T(8,128)} async-done(((f32[512,128]{1,0:T(8,128)}), f32[512,128]{1,0:T(8,128)}) %all-reduce.9.cloned.1.call-update) | async-done | bytes 262160 | tf_op jit(solution)/shard_map/while/body/eval_jaxpr/psum | solution.py:112
  1156.9 88.0 %all-reduce.7.cloned.1.call-done = f32[512,128]{1,0:T(8,128)} async-done(((f32[512,128]{1,0:T(8,128)}), f32[512,128]{1,0:T(8,128)}) %all-reduce.7.cloned.1.call-update) | async-done | bytes 262160 | tf_op jit(solution)/shard_map/while/body/eval_jaxpr/psum | solution.py:11
  1255.0 40.6 %all-reduce.9.cloned.1.call-done = f32[512,128]{1,0:T(8,128)} async-done(((f32[512,128]{1,0:T(8,128)}), f32[512,128]{1,0:T(8,128)}) %all-reduce.9.cloned.1.call-update) | async-done | bytes 262160 | tf_op jit(solution)/shard_map/while/body/eval_jaxpr/psum | solution.py:112
  1296.5 86.8 %all-reduce.7.cloned.1.call-done = f32[512,128]{1,0:T(8,128)} async-done(((f32[512,128]{1,0:T(8,128)}), f32[512,128]{1,0:T(8,128)}) %all-reduce.7.cloned.1.call-update) | async-done | bytes 262160 | tf_op jit(solution)/shard_map/while/body/eval_jaxpr/psum | solution.py:11
  1392.5 39.6 %all-reduce.9.cloned.1.call-done = f32[512,128]{1,0:T(8,128)} async-done(((f32[512,128]{1,0:T(8,128)}), f32[512,128]{1,0:T(8,128)}) %all-reduce.9.cloned.1.call-update) | async-done | bytes 262160 | tf_op jit(solution)/shard_map/while/body/eval_jaxpr/psum | solution.py:112
  1433.0 85.3 %all-reduce.7.cloned.1.call-done = f32[512,128]{1,0:T(8,128)} async-done(((f32[512,128]{1,0:T(8,128)}), f32[512,128]{1,0:T(8,128)}) %all-reduce.7.cloned.1.call-update) | async-done | bytes 262160 | tf_op jit(solution)/shard_map/while/body/eval_jaxpr/psum | solution.py:11
  1527.5 40.6 %all-reduce.9.cloned.1.call-done = f32[512,128]{1,0:T(8,128)} async-done(((f32[512,128]{1,0:T(8,128)}), f32[512,128]{1,0:T(8,128)}) %all-reduce.9.cloned.1.call-update) | async-done | bytes 262160 | tf_op jit(solution)/shard_map/while/body/eval_jaxpr/psum | solution.py:112
  1569.1 85.9 %all-reduce.7.cloned.1.call-done = f32[512,128]{1,0:T(8,128)} async-done(((f32[512,128]{1,0:T(8,128)}), f32[512,128]{1,0:T(8,128)}) %all-reduce.7.cloned.1.call-update) | async-done | bytes 262160 | tf_op jit(solution)/shard_map/while/body/eval_jaxpr/psum | solution.py:11
  1664.2 37.7 %all-reduce.9.cloned.1.call-done = f32[512,128]{1,0:T(8,128)} async-done(((f32[512,128]{1,0:T(8,128)}), f32[512,128]{1,0:T(8,128)}) %all-reduce.9.cloned.1.call-update) | async-done | bytes 262160 | tf_op jit(solution)/shard_map/while/body/eval_jaxpr/psum | solution.py:112
  1702.9 88.1 %all-reduce.7.cloned.1.call-done = f32[512,128]{1,0:T(8,128)} async-done(((f32[512,128]{1,0:T(8,128)}), f32[512,128]{1,0:T(8,128)}) %all-reduce.7.cloned.1.call-update) | async-done | bytes 262160 | tf_op jit(solution)/shard_map/while/body/eval_jaxpr/psum | solution.py:11
  1801.1 40.6 %all-reduce.9.cloned.1.call-done = f32[512,128]{1,0:T(8,128)} async-done(((f32[512,128]{1,0:T(8,128)}), f32[512,128]{1,0:T(8,128)}) %all-reduce.9.cloned.1.call-update) | async-done | bytes 262160 | tf_op jit(solution)/shard_map/while/body/eval_jaxpr/psum | solution.py:112
  1842.6 86.8 %all-reduce.7.cloned.1.call-done = f32[512,128]{1,0:T(8,128)} async-done(((f32[512,128]{1,0:T(8,128)}), f32[512,128]{1,0:T(8,128)}) %all-reduce.7.cloned.1.call-update) | async-done | bytes 262160 | tf_op jit(solution)/shard_map/while/body/eval_jaxpr/psum | solution.py:11
  1933.0 5.7 conditional.16
  1940.4 37.8 %all-reduce.9.cloned.1.call-done = f32[512,128]{1,0:T(8,128)} async-done(((f32[512,128]{1,0:T(8,128)}), f32[512,128]{1,0:T(8,128)}) %all-reduce.9.cloned.1.call-update) | async-done | bytes 262160 | tf_op jit(solution)/shard_map/while/body/eval_jaxpr/psum | solution.py:112
  1979.1 85.3 %all-reduce.7.cloned.1.call-done = f32[512,128]{1,0:T(8,128)} async-done(((f32[512,128]{1,0:T(8,128)}), f32[512,128]{1,0:T(8,128)}) %all-reduce.7.cloned.1.call-update) | async-done | bytes 262160 | tf_op jit(solution)/shard_map/while/body/eval_jaxpr/psum | solution.py:11
  2068.1 5.7 conditional.16
  2074.6 9.9 collective-permute-done
  2084.6 65.1 %conditional.15 = (f32[512,128]{1,0:T(8,128)S(1)}) conditional(s32[]{:T(128)} %convert_element_type.68, () %tuple.144, (s32[]{:T(128)}, s32[]{:T(128)}, f32[4,2,512,512]{2,3,0,1:T(8,128)}, s32[]{:T(128)}, pred[]{:T(512)}, /*index=5*/pred[]{:T(512)}, s32[]{:T(128)}, f32[2,512,128]{2,1,0:T(8,128)}, f32[512,128]{1,0:T(8,128)S(1)}, ...), branch_computations={%region_6.7_spmd, %region_7.8_spmd} | conditional | flops 252690464 | bytes 22546512 | solution.py:76
  2084.6 10.0 copy.8
  2095.9 10.6 while.27
  2106.5 40.1 %custom-call.5 = f32[4,128,128]{1,2,0:T(8,128)S(1)} custom-call(f32[4,128,128]{2,1,0:T(8,128)} %get-tuple-element.560), custom_call_target="InvertDiagBlocksLowerTriangular" | custom-call | tf_op jit(solution)/shard_map/while/body/eval_jaxpr/cond/branch_1_fun/triangular_solve/custom-call.1 | solution.py:72
  2151.5 48.9 %all-reduce.7.cloned.1.call-done = f32[512,128]{1,0:T(8,128)} async-done(((f32[512,128]{1,0:T(8,128)}), f32[512,128]{1,0:T(8,128)}) %all-reduce.7.cloned.1.call-update) | async-done | bytes 262160 | tf_op jit(solution)/shard_map/while/body/eval_jaxpr/psum | solution.py:11
  2201.4 11.0 fusion.55
  (350 shorter events, 182.1 us)
Async XLA Ops:
  7.2 2194.2 %copy-start = (f32[2,1,512,128]{3,2,1,0:T(8,128)S(1)}, f32[2,1,512,128]{3,2,1,0:T(8,128)}, u32[]{:S(2)}) copy-start(f32[2,1,512,128]{3,2,1,0:T(8,128)} %param.20) | copy-start | bytes 1572868
  7.2 145.9 %all-reduce.5.cloned.1.call-start = ((), (), s32[]{:S(2)}) async-start(), calls=%async_computation | async-start | bytes 524288 | tf_op jit(solution)/shard_map/psum | solution.py:11
  7.2 17.2 copy-start.3
  153.3 50.7 %all-reduce.9.cloned.1.call-start = ((), (), s32[]{:S(2)}) async-start(), calls=%async_computation.2 | async-start | bytes 524288 | tf_op jit(solution)/shard_map/while/body/eval_jaxpr/psum | solution.py:112
  153.4 9.1 collective-permute-start
  158.5 133.2 %all-reduce.7.cloned.1.call-start = ((), (), s32[]{:S(2)}) async-start(), calls=%async_computation.1 | async-start | bytes 524288 | tf_op jit(solution)/shard_map/while/body/eval_jaxpr/psum | solution.py:11
  291.7 48.7 %all-reduce.9.cloned.1.call-start = ((), (), s32[]{:S(2)}) async-start(), calls=%async_computation.2 | async-start | bytes 524288 | tf_op jit(solution)/shard_map/while/body/eval_jaxpr/psum | solution.py:112
  291.9 8.1 collective-permute-start
  296.0 130.7 %all-reduce.7.cloned.1.call-start = ((), (), s32[]{:S(2)}) async-start(), calls=%async_computation.1 | async-start | bytes 524288 | tf_op jit(solution)/shard_map/while/body/eval_jaxpr/psum | solution.py:11
  426.8 49.7 %all-reduce.9.cloned.1.call-start = ((), (), s32[]{:S(2)}) async-start(), calls=%async_computation.2 | async-start | bytes 524288 | tf_op jit(solution)/shard_map/while/body/eval_jaxpr/psum | solution.py:112
  426.9 8.1 collective-permute-start
  431.1 132.2 %all-reduce.7.cloned.1.call-start = ((), (), s32[]{:S(2)}) async-start(), calls=%async_computation.1 | async-start | bytes 524288 | tf_op jit(solution)/shard_map/while/body/eval_jaxpr/psum | solution.py:11
  564.3 46.0 %all-reduce.9.cloned.1.call-start = ((), (), s32[]{:S(2)}) async-start(), calls=%async_computation.2 | async-start | bytes 524288 | tf_op jit(solution)/shard_map/while/body/eval_jaxpr/psum | solution.py:112
  564.5 7.3 collective-permute-start
  567.7 131.6 %all-reduce.7.cloned.1.call-start = ((), (), s32[]{:S(2)}) async-start(), calls=%async_computation.1 | async-start | bytes 524288 | tf_op jit(solution)/shard_map/while/body/eval_jaxpr/psum | solution.py:11
  699.4 50.6 %all-reduce.9.cloned.1.call-start = ((), (), s32[]{:S(2)}) async-start(), calls=%async_computation.2 | async-start | bytes 524288 | tf_op jit(solution)/shard_map/while/body/eval_jaxpr/psum | solution.py:112
  699.5 9.1 collective-permute-start
  704.6 133.1 %all-reduce.7.cloned.1.call-start = ((), (), s32[]{:S(2)}) async-start(), calls=%async_computation.1 | async-start | bytes 524288 | tf_op jit(solution)/shard_map/while/body/eval_jaxpr/psum | solution.py:11
  837.8 48.7 %all-reduce.9.cloned.1.call-start = ((), (), s32[]{:S(2)}) async-start(), calls=%async_computation.2 | async-start | bytes 524288 | tf_op jit(solution)/shard_map/while/body/eval_jaxpr/psum | solution.py:112
  838.0 10.0 collective-permute-start
  847.8 125.0 %all-reduce.7.cloned.1.call-start = ((), (), s32[]{:S(2)}) async-start(), calls=%async_computation.1 | async-start | bytes 524288 | tf_op jit(solution)/shard_map/while/body/eval_jaxpr/psum | solution.py:11
  972.9 86.0 %all-reduce.9.cloned.1.call-start = ((), (), s32[]{:S(2)}) async-start(), calls=%async_computation.2 | async-start | bytes 524288 | tf_op jit(solution)/shard_map/while/body/eval_jaxpr/psum | solution.py:112
  973.0 19.9 collective-permute-start
  977.2 131.5 %all-reduce.7.cloned.1.call-start = ((), (), s32[]{:S(2)}) async-start(), calls=%async_computation.1 | async-start | bytes 524288 | tf_op jit(solution)/shard_map/while/body/eval_jaxpr/psum | solution.py:11
  1109.7 46.2 %all-reduce.9.cloned.1.call-start = ((), (), s32[]{:S(2)}) async-start(), calls=%async_computation.2 | async-start | bytes 524288 | tf_op jit(solution)/shard_map/while/body/eval_jaxpr/psum | solution.py:112
  1109.9 7.3 collective-permute-start
  1113.1 131.8 %all-reduce.7.cloned.1.call-start = ((), (), s32[]{:S(2)}) async-start(), calls=%async_computation.1 | async-start | bytes 524288 | tf_op jit(solution)/shard_map/while/body/eval_jaxpr/psum | solution.py:11
  1244.9 50.7 %all-reduce.9.cloned.1.call-start = ((), (), s32[]{:S(2)}) async-start(), calls=%async_computation.2 | async-start | bytes 524288 | tf_op jit(solution)/shard_map/while/body/eval_jaxpr/psum | solution.py:112
  1245.1 9.1 collective-permute-start
  1250.2 133.2 %all-reduce.7.cloned.1.call-start = ((), (), s32[]{:S(2)}) async-start(), calls=%async_computation.1 | async-start | bytes 524288 | tf_op jit(solution)/shard_map/while/body/eval_jaxpr/psum | solution.py:11
  1383.4 48.7 %all-reduce.9.cloned.1.call-start = ((), (), s32[]{:S(2)}) async-start(), calls=%async_computation.2 | async-start | bytes 524288 | tf_op jit(solution)/shard_map/while/body/eval_jaxpr/psum | solution.py:112
  1383.5 8.1 collective-permute-start
  1387.7 130.7 %all-reduce.7.cloned.1.call-start = ((), (), s32[]{:S(2)}) async-start(), calls=%async_computation.1 | async-start | bytes 524288 | tf_op jit(solution)/shard_map/while/body/eval_jaxpr/psum | solution.py:11
  1518.4 49.7 %all-reduce.9.cloned.1.call-start = ((), (), s32[]{:S(2)}) async-start(), calls=%async_computation.2 | async-start | bytes 524288 | tf_op jit(solution)/shard_map/while/body/eval_jaxpr/psum | solution.py:112
  1518.6 8.1 collective-permute-start
  1522.7 132.2 %all-reduce.7.cloned.1.call-start = ((), (), s32[]{:S(2)}) async-start(), calls=%async_computation.1 | async-start | bytes 524288 | tf_op jit(solution)/shard_map/while/body/eval_jaxpr/psum | solution.py:11
  1656.0 46.0 %all-reduce.9.cloned.1.call-start = ((), (), s32[]{:S(2)}) async-start(), calls=%async_computation.2 | async-start | bytes 524288 | tf_op jit(solution)/shard_map/while/body/eval_jaxpr/psum | solution.py:112
  1656.1 7.3 collective-permute-start
  1659.3 131.6 %all-reduce.7.cloned.1.call-start = ((), (), s32[]{:S(2)}) async-start(), calls=%async_computation.1 | async-start | bytes 524288 | tf_op jit(solution)/shard_map/while/body/eval_jaxpr/psum | solution.py:11
  1791.0 50.6 %all-reduce.9.cloned.1.call-start = ((), (), s32[]{:S(2)}) async-start(), calls=%async_computation.2 | async-start | bytes 524288 | tf_op jit(solution)/shard_map/while/body/eval_jaxpr/psum | solution.py:112
  1791.2 9.1 collective-permute-start
  1796.3 133.1 %all-reduce.7.cloned.1.call-start = ((), (), s32[]{:S(2)}) async-start(), calls=%async_computation.1 | async-start | bytes 524288 | tf_op jit(solution)/shard_map/while/body/eval_jaxpr/psum | solution.py:11
  1929.5 48.7 %all-reduce.9.cloned.1.call-start = ((), (), s32[]{:S(2)}) async-start(), calls=%async_computation.2 | async-start | bytes 524288 | tf_op jit(solution)/shard_map/while/body/eval_jaxpr/psum | solution.py:112
  1929.6 9.9 collective-permute-start
  1939.4 125.0 %all-reduce.7.cloned.1.call-start = ((), (), s32[]{:S(2)}) async-start(), calls=%async_computation.1 | async-start | bytes 524288 | tf_op jit(solution)/shard_map/while/body/eval_jaxpr/psum | solution.py:11
  2064.5 86.0 %all-reduce.9.cloned.1.call-start = ((), (), s32[]{:S(2)}) async-start(), calls=%async_computation.2 | async-start | bytes 524288 | tf_op jit(solution)/shard_map/while/body/eval_jaxpr/psum | solution.py:112
  2064.7 19.9 collective-permute-start
  2074.5 125.8 %all-reduce.7.cloned.1.call-start = ((), (), s32[]{:S(2)}) async-start(), calls=%async_computation.1 | async-start | bytes 524288 | tf_op jit(solution)/shard_map/while/body/eval_jaxpr/psum | solution.py:11
  (16 other events, 22.0 us)
Sparse Core Ops, SparseCore 0:
  35.2 117.8 all-reduce.4
  158.6 45.2 all-reduce.8
  207.6 84.0 all-reduce.6
  296.2 44.2 all-reduce.8
  343.9 82.7 all-reduce.6
  431.2 45.2 all-reduce.8
  480.1 83.1 all-reduce.6
  567.8 42.4 all-reduce.8
  614.0 85.3 all-reduce.6
  704.8 45.2 all-reduce.8
  753.7 84.0 all-reduce.6
  847.9 38.5 all-reduce.8
  890.2 82.6 all-reduce.6
  977.3 44.9 all-reduce.8
  1058.9 49.7 all-reduce.6
  1113.2 42.6 all-reduce.8
  1159.4 85.4 all-reduce.6
  1250.3 45.2 all-reduce.8
  1299.2 84.0 all-reduce.6
  1387.8 44.2 all-reduce.8
  1435.7 82.6 all-reduce.6
  1522.8 45.2 all-reduce.8
  1571.7 83.1 all-reduce.6
  1659.5 42.4 all-reduce.8
  1705.6 85.3 all-reduce.6
  1796.4 45.2 all-reduce.8
  1845.1 84.2 all-reduce.6
  1939.6 38.5 all-reduce.8
  1981.8 82.6 all-reduce.6
  2074.7 45.0 all-reduce.8
  2150.6 49.7 all-reduce.6
where the time goes:
time: 2220 us
  waiting for transfers between devices  1920 us (86%)
  other arithmetic  111 us (5%)
  local copies, waits for them, and re-layouts  84.6 us (4%)
  starting transfers between devices  53 us (2%)
  matrix products  32.1 us (1%)
    psum x16, waiting for transfers between devices, broadcast(): return lax.psum(jnp.where(mine, value, jnp.zeros_like(value)), axis)  1340 us
    psum x15, waiting for transfers between devices, sweep_step(): next_sum = lax.psum(next_partial, 'row')  512 us
    another operation x10, other arithmetic, solve_here(): lax.linalg.triangular_solve(diagonal, right_side, left_side=True, lower=T...  83 us
    ppermute x15, waiting for transfers between devices, from_behind(): lax.ppermute(value, axis, [(i, (i + by) % size) for i in range(size)])  68.5 us
    ppermute x15, starting transfers between devices, from_behind(): lax.ppermute(value, axis, [(i, (i + by) % size) for i in range(size)])  51.7 us
  transfers between devices with their start and end apart: 46, of which 42 were waited for; matrix products, arithmetic and copies ran while one was open for 8% of the time, Pallas kernels for 0%

commit v1 on v0

--- a/solution.py
+++ b/solution.py
@@ -8,7 +8,7 @@
 
 def broadcast(value, axis, root):
     mine = lax.axis_index(axis) == root
-    return lax.psum(jnp.where(mine, value, jnp.zeros_like(value)), axis)
+    return jnp.sum(lax.all_gather(jnp.where(mine, value, jnp.zeros_like(value)), axis), axis=0)
 
 
 def from_behind(value, axis, by):

time: 2220 us -> 1830 us (0.82)
  waiting for transfers between devices: 1920 us -> 1510 us
  other arithmetic: 111 us -> 135 us
    psum x16 -> x0, waiting for transfers between devices: 1340 us -> none  [broadcast(): return lax.psum(jnp.where(mine, value, jnp.zeros_like(value)), axis)]
    all_gather x0 -> x16, waiting for transfers between devices: none -> 919 us  [broadcast(): lax.all_gather(jnp.where(mine, value, jnp.zeros_like(value)), axis)]
    reduce_sum x0 -> x16, other arithmetic: none -> 27.5 us  [broadcast(): jnp.sum(lax.all_gather(jnp.where(mine, value, jnp.zeros_like(value)), axi...]
  transfers between devices with their start and end apart: 46 -> 46, of which waited for: 42 -> 42; matrix products, arithmetic and copies ran while one was open for 8% -> 9% of each run, Pallas kernels for 0% -> 0%
where the time goes in v1:
time: 1830 us
  waiting for transfers between devices  1510 us (83%)
  other arithmetic  135 us (7%)
  local copies, waits for them, and re-layouts  84.2 us (5%)
  starting transfers between devices  52 us (3%)
  matrix products  32.1 us (2%)
    all_gather x16, waiting for transfers between devices, broadcast(): lax.all_gather(jnp.where(mine, value, jnp.zeros_like(value)), axis)  919 us
    psum x15, waiting for transfers between devices, sweep_step(): next_sum = lax.psum(next_partial, 'row')  507 us
    another operation x10, other arithmetic, solve_here(): lax.linalg.triangular_solve(diagonal, right_side, left_side=True, lower=T...  83 us
    ppermute x15, waiting for transfers between devices, from_behind(): lax.ppermute(value, axis, [(i, (i + by) % size) for i in range(size)])  79.5 us
    ppermute x15, starting transfers between devices, from_behind(): lax.ppermute(value, axis, [(i, (i + by) % size) for i in range(size)])  50.7 us
  transfers between devices with their start and end apart: 46, of which 42 were waited for; matrix products, arithmetic and copies ran while one was open for 9% of the time, Pallas kernels for 0%

profile of v1, /device:TPU:0, one launch (start us, length us, event | category | flops | bytes accessed | tf_op | source)
XLA Modules:
  0.0 1828.8 jit_solution(14196743532766641498)
XLA Ops:
  8.1 9.9 copy.12
  18.0 7.3 copy.11
  25.3 9.6 convert_select_fusion
  36.8 91.1 %all-gather.9.cloned.1.call-done = f32[4096,128]{1,0:T(8,128)} async-done(((f32[512,128]{1,0:T(8,128)}), f32[4096,128]{1,0:T(8,128)}) %all-gather.9.cloned.1.call-update) | async-done | bytes 2097168 | tf_op jit(solution)/shard_map/all_gather | solution.py:11
  129.7 1680.7 %while.28 = (s32[]{:T(128)}, f32[4,512,128]{2,1,0:T(8,128)S(1)}, f32[512,128]{1,0:T(8,128)S(1)}, s32[]{:T(128)}, s32[]{:T(128)}, /*index=5*/f32[4,2,512,512]{2,3...) while((s32[]{:T(128)}, f32[4,512,128]{2,1,0:T(8,128)S(1)}, ...), condition=%wide.region_12.14_spmd.clone.clone, body=%wide.region_3.13_spmd.clone.clone.sunk | while | flops 2266873856 | bytes 61345600 | solution.py:116
  140.0 40.0 %all-reduce.3.cloned.1.call-done = f32[512,128]{1,0:T(8,128)} async-done(((f32[512,128]{1,0:T(8,128)}), f32[512,128]{1,0:T(8,128)}) %all-reduce.3.cloned.1.call-update) | async-done | bytes 262160 | tf_op jit(solution)/shard_map/while/body/eval_jaxpr/psum | solution.py:112
  181.0 60.5 %all-gather.11.cloned.1.call-done = f32[4096,128]{1,0:T(8,128)} async-done(((f32[512,128]{1,0:T(8,128)}), f32[4096,128]{1,0:T(8,128)}) %all-gather.11.cloned.1.call-update) | async-done | bytes 2097168 | tf_op jit(solution)/shard_map/while/body/eval_jaxpr/all_gather | solution.py:11
  253.6 39.5 %all-reduce.3.cloned.1.call-done = f32[512,128]{1,0:T(8,128)} async-done(((f32[512,128]{1,0:T(8,128)}), f32[512,128]{1,0:T(8,128)}) %all-reduce.3.cloned.1.call-update) | async-done | bytes 262160 | tf_op jit(solution)/shard_map/while/body/eval_jaxpr/psum | solution.py:112
  294.1 59.0 %all-gather.11.cloned.1.call-done = f32[4096,128]{1,0:T(8,128)} async-done(((f32[512,128]{1,0:T(8,128)}), f32[4096,128]{1,0:T(8,128)}) %all-gather.11.cloned.1.call-update) | async-done | bytes 2097168 | tf_op jit(solution)/shard_map/while/body/eval_jaxpr/all_gather | solution.py:11
  365.1 39.0 %all-reduce.3.cloned.1.call-done = f32[512,128]{1,0:T(8,128)} async-done(((f32[512,128]{1,0:T(8,128)}), f32[512,128]{1,0:T(8,128)}) %all-reduce.3.cloned.1.call-update) | async-done | bytes 262160 | tf_op jit(solution)/shard_map/while/body/eval_jaxpr/psum | solution.py:112
  405.1 59.7 %all-gather.11.cloned.1.call-done = f32[4096,128]{1,0:T(8,128)} async-done(((f32[512,128]{1,0:T(8,128)}), f32[4096,128]{1,0:T(8,128)}) %all-gather.11.cloned.1.call-update) | async-done | bytes 2097168 | tf_op jit(solution)/shard_map/while/body/eval_jaxpr/all_gather | solution.py:11
  476.8 37.8 %all-reduce.3.cloned.1.call-done = f32[512,128]{1,0:T(8,128)} async-done(((f32[512,128]{1,0:T(8,128)}), f32[512,128]{1,0:T(8,128)}) %all-reduce.3.cloned.1.call-update) | async-done | bytes 262160 | tf_op jit(solution)/shard_map/while/body/eval_jaxpr/psum | solution.py:112
  515.5 61.7 %all-gather.11.cloned.1.call-done = f32[4096,128]{1,0:T(8,128)} async-done(((f32[512,128]{1,0:T(8,128)}), f32[4096,128]{1,0:T(8,128)}) %all-gather.11.cloned.1.call-update) | async-done | bytes 2097168 | tf_op jit(solution)/shard_map/while/body/eval_jaxpr/all_gather | solution.py:11
  589.4 40.0 %all-reduce.3.cloned.1.call-done = f32[512,128]{1,0:T(8,128)} async-done(((f32[512,128]{1,0:T(8,128)}), f32[512,128]{1,0:T(8,128)}) %all-reduce.3.cloned.1.call-update) | async-done | bytes 262160 | tf_op jit(solution)/shard_map/while/body/eval_jaxpr/psum | solution.py:112
  630.4 60.5 %all-gather.11.cloned.1.call-done = f32[4096,128]{1,0:T(8,128)} async-done(((f32[512,128]{1,0:T(8,128)}), f32[4096,128]{1,0:T(8,128)}) %all-gather.11.cloned.1.call-update) | async-done | bytes 2097168 | tf_op jit(solution)/shard_map/while/body/eval_jaxpr/all_gather | solution.py:11
  696.2 5.7 conditional.16
  696.2 5.7 fusion.11
  703.6 38.1 %all-reduce.3.cloned.1.call-done = f32[512,128]{1,0:T(8,128)} async-done(((f32[512,128]{1,0:T(8,128)}), f32[512,128]{1,0:T(8,128)}) %all-reduce.3.cloned.1.call-update) | async-done | bytes 262160 | tf_op jit(solution)/shard_map/while/body/eval_jaxpr/psum | solution.py:112
  742.6 59.0 %all-gather.11.cloned.1.call-done = f32[4096,128]{1,0:T(8,128)} async-done(((f32[512,128]{1,0:T(8,128)}), f32[4096,128]{1,0:T(8,128)}) %all-gather.11.cloned.1.call-update) | async-done | bytes 2097168 | tf_op jit(solution)/shard_map/while/body/eval_jaxpr/all_gather | solution.py:11
  807.9 14.6 collective-permute-done
  822.5 65.2 %conditional.15 = (f32[512,128]{1,0:T(8,128)S(1)}) conditional(s32[]{:T(128)} %convert_element_type.68, () %tuple.144, (s32[]{:T(128)}, s32[]{:T(128)}, f32[4,2,512,512]{2,3,0,1:T(8,128)}, s32[]{:T(128)}, pred[]{:T(512)}, /*index=5*/pred[]{:T(512)}, s32[]{:T(128)}, f32[2,512,128]{2,1,0:T(8,128)}, f32[512,128]{1,0:T(8,128)S(1)}, ...), branch_computations={%region_6.7_spmd, %region_7.8_spmd} | conditional | flops 252690464 | bytes 22546512 | solution.py:76
  822.5 10.0 copy.8
  833.8 10.6 while.27
  844.4 40.1 %custom-call.5 = f32[4,128,128]{1,2,0:T(8,128)S(1)} custom-call(f32[4,128,128]{2,1,0:T(8,128)} %get-tuple-element.560), custom_call_target="InvertDiagBlocksLowerTriangular" | custom-call | tf_op jit(solution)/shard_map/while/body/eval_jaxpr/cond/branch_1_fun/triangular_solve/custom-call.1 | solution.py:72
  889.4 22.6 %all-gather.11.cloned.1.call-done = f32[4096,128]{1,0:T(8,128)} async-done(((f32[512,128]{1,0:T(8,128)}), f32[4096,128]{1,0:T(8,128)}) %all-gather.11.cloned.1.call-update) | async-done | bytes 2097168 | tf_op jit(solution)/shard_map/while/body/eval_jaxpr/all_gather | solution.py:11
  924.1 37.7 %all-reduce.3.cloned.1.call-done = f32[512,128]{1,0:T(8,128)} async-done(((f32[512,128]{1,0:T(8,128)}), f32[512,128]{1,0:T(8,128)}) %all-reduce.3.cloned.1.call-update) | async-done | bytes 262160 | tf_op jit(solution)/shard_map/while/body/eval_jaxpr/psum | solution.py:112
  962.8 61.7 %all-gather.11.cloned.1.call-done = f32[4096,128]{1,0:T(8,128)} async-done(((f32[512,128]{1,0:T(8,128)}), f32[4096,128]{1,0:T(8,128)}) %all-gather.11.cloned.1.call-update) | async-done | bytes 2097168 | tf_op jit(solution)/shard_map/while/body/eval_jaxpr/all_gather | solution.py:11
  1036.6 40.0 %all-reduce.3.cloned.1.call-done = f32[512,128]{1,0:T(8,128)} async-done(((f32[512,128]{1,0:T(8,128)}), f32[512,128]{1,0:T(8,128)}) %all-reduce.3.cloned.1.call-update) | async-done | bytes 262160 | tf_op jit(solution)/shard_map/while/body/eval_jaxpr/psum | solution.py:112
  1077.5 60.5 %all-gather.11.cloned.1.call-done = f32[4096,128]{1,0:T(8,128)} async-done(((f32[512,128]{1,0:T(8,128)}), f32[4096,128]{1,0:T(8,128)}) %all-gather.11.cloned.1.call-update) | async-done | bytes 2097168 | tf_op jit(solution)/shard_map/while/body/eval_jaxpr/all_gather | solution.py:11
  1150.2 39.5 %all-reduce.3.cloned.1.call-done = f32[512,128]{1,0:T(8,128)} async-done(((f32[512,128]{1,0:T(8,128)}), f32[512,128]{1,0:T(8,128)}) %all-reduce.3.cloned.1.call-update) | async-done | bytes 262160 | tf_op jit(solution)/shard_map/while/body/eval_jaxpr/psum | solution.py:112
  1190.7 59.0 %all-gather.11.cloned.1.call-done = f32[4096,128]{1,0:T(8,128)} async-done(((f32[512,128]{1,0:T(8,128)}), f32[4096,128]{1,0:T(8,128)}) %all-gather.11.cloned.1.call-update) | async-done | bytes 2097168 | tf_op jit(solution)/shard_map/while/body/eval_jaxpr/all_gather | solution.py:11
  1261.7 39.0 %all-reduce.3.cloned.1.call-done = f32[512,128]{1,0:T(8,128)} async-done(((f32[512,128]{1,0:T(8,128)}), f32[512,128]{1,0:T(8,128)}) %all-reduce.3.cloned.1.call-update) | async-done | bytes 262160 | tf_op jit(solution)/shard_map/while/body/eval_jaxpr/psum | solution.py:112
  1301.7 59.7 %all-gather.11.cloned.1.call-done = f32[4096,128]{1,0:T(8,128)} async-done(((f32[512,128]{1,0:T(8,128)}), f32[4096,128]{1,0:T(8,128)}) %all-gather.11.cloned.1.call-update) | async-done | bytes 2097168 | tf_op jit(solution)/shard_map/while/body/eval_jaxpr/all_gather | solution.py:11
  1373.4 37.8 %all-reduce.3.cloned.1.call-done = f32[512,128]{1,0:T(8,128)} async-done(((f32[512,128]{1,0:T(8,128)}), f32[512,128]{1,0:T(8,128)}) %all-reduce.3.cloned.1.call-update) | async-done | bytes 262160 | tf_op jit(solution)/shard_map/while/body/eval_jaxpr/psum | solution.py:112
  1412.1 61.7 %all-gather.11.cloned.1.call-done = f32[4096,128]{1,0:T(8,128)} async-done(((f32[512,128]{1,0:T(8,128)}), f32[4096,128]{1,0:T(8,128)}) %all-gather.11.cloned.1.call-update) | async-done | bytes 2097168 | tf_op jit(solution)/shard_map/while/body/eval_jaxpr/all_gather | solution.py:11
  1486.0 40.0 %all-reduce.3.cloned.1.call-done = f32[512,128]{1,0:T(8,128)} async-done(((f32[512,128]{1,0:T(8,128)}), f32[512,128]{1,0:T(8,128)}) %all-reduce.3.cloned.1.call-update) | async-done | bytes 262160 | tf_op jit(solution)/shard_map/while/body/eval_jaxpr/psum | solution.py:112
  1527.0 60.5 %all-gather.11.cloned.1.call-done = f32[4096,128]{1,0:T(8,128)} async-done(((f32[512,128]{1,0:T(8,128)}), f32[4096,128]{1,0:T(8,128)}) %all-gather.11.cloned.1.call-update) | async-done | bytes 2097168 | tf_op jit(solution)/shard_map/while/body/eval_jaxpr/all_gather | solution.py:11
  1592.8 5.7 conditional.16
  1600.2 38.1 %all-reduce.3.cloned.1.call-done = f32[512,128]{1,0:T(8,128)} async-done(((f32[512,128]{1,0:T(8,128)}), f32[512,128]{1,0:T(8,128)}) %all-reduce.3.cloned.1.call-update) | async-done | bytes 262160 | tf_op jit(solution)/shard_map/while/body/eval_jaxpr/psum | solution.py:112
  1639.2 59.0 %all-gather.11.cloned.1.call-done = f32[4096,128]{1,0:T(8,128)} async-done(((f32[512,128]{1,0:T(8,128)}), f32[4096,128]{1,0:T(8,128)}) %all-gather.11.cloned.1.call-update) | async-done | bytes 2097168 | tf_op jit(solution)/shard_map/while/body/eval_jaxpr/all_gather | solution.py:11
  1703.6 5.7 conditional.16
  1710.1 9.0 collective-permute-done
  1719.1 65.1 %conditional.15 = (f32[512,128]{1,0:T(8,128)S(1)}) conditional(s32[]{:T(128)} %convert_element_type.68, () %tuple.144, (s32[]{:T(128)}, s32[]{:T(128)}, f32[4,2,512,512]{2,3,0,1:T(8,128)}, s32[]{:T(128)}, pred[]{:T(512)}, /*index=5*/pred[]{:T(512)}, s32[]{:T(128)}, f32[2,512,128]{2,1,0:T(8,128)}, f32[512,128]{1,0:T(8,128)S(1)}, ...), branch_computations={%region_6.7_spmd, %region_7.8_spmd} | conditional | flops 252690464 | bytes 22546512 | solution.py:76
  1719.1 10.0 copy.8
  1730.4 10.6 while.27
  1741.0 40.1 %custom-call.5 = f32[4,128,128]{1,2,0:T(8,128)S(1)} custom-call(f32[4,128,128]{2,1,0:T(8,128)} %get-tuple-element.560), custom_call_target="InvertDiagBlocksLowerTriangular" | custom-call | tf_op jit(solution)/shard_map/while/body/eval_jaxpr/cond/branch_1_fun/triangular_solve/custom-call.1 | solution.py:72
  1786.0 22.6 %all-gather.11.cloned.1.call-done = f32[4096,128]{1,0:T(8,128)} async-done(((f32[512,128]{1,0:T(8,128)}), f32[4096,128]{1,0:T(8,128)}) %all-gather.11.cloned.1.call-update) | async-done | bytes 2097168 | tf_op jit(solution)/shard_map/while/body/eval_jaxpr/all_gather | solution.py:11
  1810.4 11.0 fusion.56
  (351 shorter events, 217.7 us)
Async XLA Ops:
  8.0 1802.4 %copy-start = (f32[2,1,512,128]{3,2,1,0:T(8,128)S(1)}, f32[2,1,512,128]{3,2,1,0:T(8,128)}, u32[]{:S(2)}) copy-start(f32[2,1,512,128]{3,2,1,0:T(8,128)} %param.20) | copy-start | bytes 1572868
  8.0 119.8 %all-gather.9.cloned.1.call-start = ((), (), s32[]{:S(2)}) async-start(), calls=%async_computation | async-start | bytes 2359296 | tf_op jit(solution)/shard_map/all_gather | solution.py:11
  8.1 17.2 copy-start.3
  129.7 50.3 %all-reduce.3.cloned.1.call-start = ((), (), s32[]{:S(2)}) async-start(), calls=%async_computation.2 | async-start | bytes 524288 | tf_op jit(solution)/shard_map/while/body/eval_jaxpr/psum | solution.py:112
  129.8 9.3 collective-permute-start
  134.0 107.5 %all-gather.11.cloned.1.call-start = ((), (), s32[]{:S(2)}) async-start(), calls=%async_computation.1 | async-start | bytes 2359296 | tf_op jit(solution)/shard_map/while/body/eval_jaxpr/all_gather | solution.py:11
  243.3 49.8 %all-reduce.3.cloned.1.call-start = ((), (), s32[]{:S(2)}) async-start(), calls=%async_computation.2 | async-start | bytes 524288 | tf_op jit(solution)/shard_map/while/body/eval_jaxpr/psum | solution.py:112
  243.4 9.3 collective-permute-start
  247.6 105.5 %all-gather.11.cloned.1.call-start = ((), (), s32[]{:S(2)}) async-start(), calls=%async_computation.1 | async-start | bytes 2359296 | tf_op jit(solution)/shard_map/while/body/eval_jaxpr/all_gather | solution.py:11
  354.9 49.3 %all-reduce.3.cloned.1.call-start = ((), (), s32[]{:S(2)}) async-start(), calls=%async_computation.2 | async-start | bytes 524288 | tf_op jit(solution)/shard_map/while/body/eval_jaxpr/psum | solution.py:112
  355.0 9.3 collective-permute-start
  359.2 105.6 %all-gather.11.cloned.1.call-start = ((), (), s32[]{:S(2)}) async-start(), calls=%async_computation.1 | async-start | bytes 2359296 | tf_op jit(solution)/shard_map/while/body/eval_jaxpr/all_gather | solution.py:11
  466.6 48.0 %all-reduce.3.cloned.1.call-start = ((), (), s32[]{:S(2)}) async-start(), calls=%async_computation.2 | async-start | bytes 524288 | tf_op jit(solution)/shard_map/while/body/eval_jaxpr/psum | solution.py:112
  466.7 9.3 collective-permute-start
  470.9 106.4 %all-gather.11.cloned.1.call-start = ((), (), s32[]{:S(2)}) async-start(), calls=%async_computation.1 | async-start | bytes 2359296 | tf_op jit(solution)/shard_map/while/body/eval_jaxpr/all_gather | solution.py:11
  579.1 50.3 %all-reduce.3.cloned.1.call-start = ((), (), s32[]{:S(2)}) async-start(), calls=%async_computation.2 | async-start | bytes 524288 | tf_op jit(solution)/shard_map/while/body/eval_jaxpr/psum | solution.py:112
  579.2 9.3 collective-permute-start
  583.4 107.5 %all-gather.11.cloned.1.call-start = ((), (), s32[]{:S(2)}) async-start(), calls=%async_computation.1 | async-start | bytes 2359296 | tf_op jit(solution)/shard_map/while/body/eval_jaxpr/all_gather | solution.py:11
  692.7 49.0 %all-reduce.3.cloned.1.call-start = ((), (), s32[]{:S(2)}) async-start(), calls=%async_computation.2 | async-start | bytes 524288 | tf_op jit(solution)/shard_map/while/body/eval_jaxpr/psum | solution.py:112
  692.8 9.9 collective-permute-start
  702.7 99.0 %all-gather.11.cloned.1.call-start = ((), (), s32[]{:S(2)}) async-start(), calls=%async_computation.1 | async-start | bytes 2359296 | tf_op jit(solution)/shard_map/while/body/eval_jaxpr/all_gather | solution.py:11
  803.4 85.0 %all-reduce.3.cloned.1.call-start = ((), (), s32[]{:S(2)}) async-start(), calls=%async_computation.2 | async-start | bytes 524288 | tf_op jit(solution)/shard_map/while/body/eval_jaxpr/psum | solution.py:112
  803.6 18.9 %collective-permute-start = (f32[512,128]{1,0:T(8,128)S(1)}, f32[512,128]{1,0:T(8,128)S(1)}, u32[]{:S(2)}, u32[]{:S(2)}) collective-permute-start(f32[512,128]{1,0:T(8,128)S(1)} %get-tuple-element.813), channel_id=1, source_target_pairs={{0,24},{8,0},{16,8},{24,16},{1,25},{9,1},{17,9},{25,17},{2,26},{10... | collective-permute-start | bytes 786440 | tf_op jit(solution)/shard_map/while/body/eval_jaxpr/ppermute | solution.py:16
  807.8 104.3 %all-gather.11.cloned.1.call-start = ((), (), s32[]{:S(2)}) async-start(), calls=%async_computation.1 | async-start | bytes 2359296 | tf_op jit(solution)/shard_map/while/body/eval_jaxpr/all_gather | solution.py:11
  913.8 48.0 %all-reduce.3.cloned.1.call-start = ((), (), s32[]{:S(2)}) async-start(), calls=%async_computation.2 | async-start | bytes 524288 | tf_op jit(solution)/shard_map/while/body/eval_jaxpr/psum | solution.py:112
  914.0 9.3 collective-permute-start
  918.1 106.4 %all-gather.11.cloned.1.call-start = ((), (), s32[]{:S(2)}) async-start(), calls=%async_computation.1 | async-start | bytes 2359296 | tf_op jit(solution)/shard_map/while/body/eval_jaxpr/all_gather | solution.py:11
  1026.3 50.3 %all-reduce.3.cloned.1.call-start = ((), (), s32[]{:S(2)}) async-start(), calls=%async_computation.2 | async-start | bytes 524288 | tf_op jit(solution)/shard_map/while/body/eval_jaxpr/psum | solution.py:112
  1026.4 9.3 collective-permute-start
  1030.6 107.5 %all-gather.11.cloned.1.call-start = ((), (), s32[]{:S(2)}) async-start(), calls=%async_computation.1 | async-start | bytes 2359296 | tf_op jit(solution)/shard_map/while/body/eval_jaxpr/all_gather | solution.py:11
  1139.9 49.8 %all-reduce.3.cloned.1.call-start = ((), (), s32[]{:S(2)}) async-start(), calls=%async_computation.2 | async-start | bytes 524288 | tf_op jit(solution)/shard_map/while/body/eval_jaxpr/psum | solution.py:112
  1140.0 9.3 collective-permute-start
  1144.2 105.5 %all-gather.11.cloned.1.call-start = ((), (), s32[]{:S(2)}) async-start(), calls=%async_computation.1 | async-start | bytes 2359296 | tf_op jit(solution)/shard_map/while/body/eval_jaxpr/all_gather | solution.py:11
  1251.4 49.3 %all-reduce.3.cloned.1.call-start = ((), (), s32[]{:S(2)}) async-start(), calls=%async_computation.2 | async-start | bytes 524288 | tf_op jit(solution)/shard_map/while/body/eval_jaxpr/psum | solution.py:112
  1251.6 9.3 collective-permute-start
  1255.8 105.6 %all-gather.11.cloned.1.call-start = ((), (), s32[]{:S(2)}) async-start(), calls=%async_computation.1 | async-start | bytes 2359296 | tf_op jit(solution)/shard_map/while/body/eval_jaxpr/all_gather | solution.py:11
  1363.1 48.0 %all-reduce.3.cloned.1.call-start = ((), (), s32[]{:S(2)}) async-start(), calls=%async_computation.2 | async-start | bytes 524288 | tf_op jit(solution)/shard_map/while/body/eval_jaxpr/psum | solution.py:112
  1363.3 9.3 collective-permute-start
  1367.5 106.4 %all-gather.11.cloned.1.call-start = ((), (), s32[]{:S(2)}) async-start(), calls=%async_computation.1 | async-start | bytes 2359296 | tf_op jit(solution)/shard_map/while/body/eval_jaxpr/all_gather | solution.py:11
  1475.7 50.3 %all-reduce.3.cloned.1.call-start = ((), (), s32[]{:S(2)}) async-start(), calls=%async_computation.2 | async-start | bytes 524288 | tf_op jit(solution)/shard_map/while/body/eval_jaxpr/psum | solution.py:112
  1475.8 9.3 collective-permute-start
  1480.0 107.5 %all-gather.11.cloned.1.call-start = ((), (), s32[]{:S(2)}) async-start(), calls=%async_computation.1 | async-start | bytes 2359296 | tf_op jit(solution)/shard_map/while/body/eval_jaxpr/all_gather | solution.py:11
  1589.3 49.0 %all-reduce.3.cloned.1.call-start = ((), (), s32[]{:S(2)}) async-start(), calls=%async_computation.2 | async-start | bytes 524288 | tf_op jit(solution)/shard_map/while/body/eval_jaxpr/psum | solution.py:112
  1589.4 9.9 collective-permute-start
  1599.3 99.0 %all-gather.11.cloned.1.call-start = ((), (), s32[]{:S(2)}) async-start(), calls=%async_computation.1 | async-start | bytes 2359296 | tf_op jit(solution)/shard_map/while/body/eval_jaxpr/all_gather | solution.py:11
  1700.0 85.0 %all-reduce.3.cloned.1.call-start = ((), (), s32[]{:S(2)}) async-start(), calls=%async_computation.2 | async-start | bytes 524288 | tf_op jit(solution)/shard_map/while/body/eval_jaxpr/psum | solution.py:112
  1700.2 18.9 %collective-permute-start = (f32[512,128]{1,0:T(8,128)S(1)}, f32[512,128]{1,0:T(8,128)S(1)}, u32[]{:S(2)}, u32[]{:S(2)}) collective-permute-start(f32[512,128]{1,0:T(8,128)S(1)} %get-tuple-element.813), channel_id=1, source_target_pairs={{0,24},{8,0},{16,8},{24,16},{1,25},{9,1},{17,9},{25,17},{2,26},{10... | collective-permute-start | bytes 786440 | tf_op jit(solution)/shard_map/while/body/eval_jaxpr/ppermute | solution.py:16
  1710.0 98.6 %all-gather.11.cloned.1.call-start = ((), (), s32[]{:S(2)}) async-start(), calls=%async_computation.1 | async-start | bytes 2359296 | tf_op jit(solution)/shard_map/while/body/eval_jaxpr/all_gather | solution.py:11
  (16 other events, 22.0 us)
Sparse Core Ops, SparseCore 0:
  36.0 91.7 all-gather.8
  134.1 45.8 all-reduce.2
  247.7 45.3 all-reduce.2
  359.3 44.8 all-reduce.2
  471.0 43.5 all-reduce.2
  583.5 45.8 all-reduce.2
  702.8 38.8 all-reduce.2
  807.9 44.0 all-reduce.2
  918.2 43.5 all-reduce.2
  1030.7 45.8 all-reduce.2
  1144.3 45.3 all-reduce.2
  1255.9 44.8 all-reduce.2
  1367.6 43.5 all-reduce.2
  1480.1 45.8 all-reduce.2
  1599.4 38.8 all-reduce.2
  1710.1 44.1 all-reduce.2
Sparse Core Ops, SparseCore 1:
  140.1 101.4 all-gather.10
  253.6 99.4 all-gather.10
  365.2 99.5 all-gather.10
  476.9 100.3 all-gather.10
  589.4 101.4 all-gather.10
  705.9 95.7 all-gather.10
  888.5 23.5 all-gather.10
  924.2 100.3 all-gather.10
  1036.6 101.4 all-gather.10
  1150.2 99.4 all-gather.10
  1261.8 99.5 all-gather.10
  1373.5 100.3 all-gather.10
  1486.0 101.4 all-gather.10
  1602.5 95.7 all-gather.10
  1785.1 23.5 all-gather.10
